TPU v7x, 32 devices: a whole 2x2x4 slice. The times are simulated.
32 devices in a mesh: date: 8 (over z, core), pix: 4 (over y, x).
Axes of the slice: x: 2, y: 2, z: 4, core: 2. Of those that a mesh axis runs over, the one named last changes fastest.
Arguments:
- bin_index: int32 [128, 262144], P('date', 'pix'), may hold values from 0 to 511
- clear_mask: bfloat16 [128, 262144], P('date', 'pix'), may hold values from 0 to 1, as said below
Outputs:
- anomaly: float32 [3, 2048], P(None, 'pix')
- tile_levels: float32 [3], replicated
Inputs may be any that keep to these rules, and one draw needn't show every extreme that they name: `clear_mask`: 0 for a cloudy observation, else a positive weight.
All inputs are finite; a program needn't handle non-finite values.
Results may differ from a plain program's by a relative error of at most 0.0003.
Values sent between devices are 32-bit elements; how exact they have to be, the bound alone decides.
No kernel may reach another device: no remote copies, remote signals or barrier semaphores. Data moves between devices by JAX's collectives and lax.ppermute only.
A program may use at most 64 MiB of HBM per device.

v0:
```python
import jax
import jax.numpy as jnp
from jax import lax
from jax.sharding import PartitionSpec as P

BINS = 512
BLOCK = 128
QUANTILES = (0.1, 0.5, 0.9)
LOW_EDGE = -1.0


def percentiles(counts, before, totals):
    target = jnp.stack([quantile * totals + 0.25 for quantile in QUANTILES])
    passed = jnp.clip(
        (target[:, :, None] - before[None]) / jnp.maximum(counts, 1.0)[None], 0.0, 1.0
    )
    return LOW_EDGE + 2.0 / BINS * jnp.sum(passed, axis=2)


def block_counts(bin_index, clear_mask, blocks):
    chosen = bin_index
    frames = chosen.shape[0]
    chosen = jnp.moveaxis(chosen.reshape(frames, blocks, BLOCK), 1, 0)
    weight = jnp.moveaxis(clear_mask.reshape(frames, blocks, BLOCK), 1, 0)
    upper_digit = chosen // 16
    lower_digit = chosen % 16
    upper_values = jnp.arange(BINS // 16, dtype=jnp.int32)
    lower_values = jnp.arange(16, dtype=jnp.int32)
    upper_table = jnp.where(
        upper_digit[:, None] == upper_values[None, :, None, None],
        weight[:, None],
        jnp.zeros((), jnp.bfloat16),
    )
    lower_table = (lower_digit[:, None] == lower_values[None, :, None, None]).astype(jnp.bfloat16)
    joint_counts = jnp.einsum(
        "ghdp,gldp->ghl", upper_table, lower_table, preferred_element_type=jnp.float32
    )
    return joint_counts.reshape(blocks, BINS)


def body(bin_index, clear_mask):
    date_devices = lax.axis_size("date")
    blocks_here = bin_index.shape[1] // BLOCK
    owned_rows = blocks_here // date_devices
    triangle = (jnp.arange(BINS)[:, None] < jnp.arange(BINS)[None, :]).astype(jnp.float32)
    owned_sums = lax.psum_scatter(
        block_counts(bin_index, clear_mask, owned_rows * lax.axis_size("date")),
        "date",
        scatter_dimension=0,
        tiled=True,
    )
    tile_counts = lax.psum(jnp.sum(owned_sums, axis=0), ("date", "pix"))
    tile_before = jnp.cumsum(tile_counts) - tile_counts
    tile_levels = percentiles(tile_counts[None], tile_before[None], jnp.sum(tile_counts)[None])[
        :, 0
    ]
    before = jnp.dot(owned_sums, triangle, precision=lax.Precision.HIGHEST)
    owned_levels = (
        percentiles(owned_sums, before, jnp.sum(owned_sums, axis=1)) - tile_levels[:, None]
    )
    anomaly = lax.all_gather(owned_levels, "date", axis=1, tiled=True)
    return (anomaly, tile_levels)


def solution(mesh):
    placed = (P("date", "pix"), P("date", "pix"))
    return jax.shard_map(
        body, mesh=mesh, in_specs=placed, out_specs=(P(None, "pix"), P()), check_vma=False
    )
```

profile of v0, /device:TPU:0, one launch (start us, length us, event | category | flops | bytes accessed | tf_op | source)
XLA Modules:
  0.0 145.4 jit_solution(10991119551946988317)
XLA Ops:
  7.2 0.0 reduce-scatter.4.cloned.1.call-start
  7.2 3.0 %copy.40 = s32[2,8,512,128]{3,2,1,0:T(8,128)S(1)} copy(s32[2,8,512,128]{3,1,2,0:T(8,128)} %bitcast.84) | data formatting | bytes 8388608
  10.2 3.8 %add_select_fusion.1 = (s32[512,16,128]{2,0,1:T(8,128)S(1)}, s32[512,16,128]{2,0,1:T(8,128)S(1)}) fusion(s32[2,8,512,128]{3,2,1,0:T(8,128)S(1)} %copy.40), kind=kLoop, calls=%fused_computation.9 | loop fusion | flops 19922944 | bytes 12582912 | tf_op jit(solution)/shard_map/jit(floor_divide)/jit(_where)/select_n | solution.py:25
  14.1 2.4 %copy.29 = s32[512,16,128]{2,1,0:T(8,128)S(1)} copy(s32[512,16,128]{2,0,1:T(8,128)S(1)} %get-tuple-element.4) | data formatting | bytes 8388608 | tf_op jit(solution)/shard_map/jit(floor_divide)/jit(_where)/select_n | solution.py:25
  16.5 0.0 copy-start
  16.5 2.4 %copy.31 = s32[512,16,128]{2,1,0:T(8,128)S(1)} copy(s32[512,16,128]{2,0,1:T(8,128)S(1)} %get-tuple-element.5) | data formatting | bytes 8388608 | tf_op jit(solution)/shard_map/jit(remainder)/select_n | solution.py:26
  18.9 0.0 copy-done
  19.0 0.4 copy.41
  19.3 1.4 copy.30
  20.7 20.1 %fusion.10 = f32[512,32,16]{1,2,0:T(8,128)} fusion(s32[512,16,128]{2,1,0:T(8,128)S(1)} %copy.31, s32[512,16,128]{2,1,0:T(8,128)S(1)} %copy.29, bf16[512,16,128]{2,1,0:T(8,128)(2,1)S(1)} %copy.30), kind=kOutput, calls=%fused_computation.18 | convolution fusion | flops 1157627904 | bytes 11534336 | tf_op jit(solution)/shard_map/ghdp,gldp->ghl/dot_general | solution.py:35
  40.8 3.2 %copy.32 = f32[512,32,16]{0,2,1:T(8,128)S(1)} copy(f32[512,32,16]{1,2,0:T(8,128)} %fusion.10) | data formatting | bytes 2097152 | tf_op jit(solution)/shard_map/ghdp,gldp->ghl/dot_general | solution.py:35
  44.0 1.3 copy.36
  45.4 0.0 reduce-scatter.4.cloned.1.call-update
  45.4 35.8 %reduce-scatter.4.cloned.1.call-done = f32[64,512]{1,0:T(8,128)} async-done(((f32[512,512]{1,0:T(8,128)}), f32[64,512]{1,0:T(8,128)}) %reduce-scatter.4.cloned.1.call-update) | async-done | bytes 131088
  81.2 1.0 fusion.15
  82.2 37.4 %psum.7 = f32[512]{0:T(512)S(1)} all-reduce(f32[512]{0:T(512)S(1)} %get-tuple-element.2), channel_id=1, replica_groups=mesh['date'=8,'pix'=4] {'date','pix'}, use_global_device_ids=true, to_apply=%region_4.5 | all-reduce | flops 512 | bytes 4096 | tf_op jit(solution)/shard_map/psum | solution.py:52
  119.6 0.3 reduce-window.9
  119.9 0.1 slice.7
  120.1 0.1 slice_reduce_fusion
  120.2 0.6 fusion.16
  122.7 0.1 maximum_bitcast_fusion
  122.8 0.2 clamp_reduce_fusion.1
  123.0 0.0 copy-start.1
  123.0 1.3 fusion.13
  124.3 0.2 clamp_reduce_fusion
  124.5 0.1 subtract_bitcast_fusion
  124.6 13.3 %all-gather = f32[8,64,3]{1,2,0:T(4,128)S(1)} all-gather(f32[1,64,3]{1,2,0:T(4,128)S(1)} %subtract_bitcast_fusion), channel_id=1, replica_groups=mesh['date'=8,'pix'=4] {'date'}, dimensions={0}, use_global_device_ids=true | all-gather | bytes 6912 | tf_op jit(solution)/shard_map/all_gather | solution.py:61
  137.9 0.7 reshape.186
  138.6 0.0 copy-done.1
  (5 shorter events, 0.1 us)
Async XLA Ops:
  7.2 74.0 %reduce-scatter.4.cloned.1.call-start = ((), (), s32[]{:S(2)}) async-start(), calls=%async_computation.1 | async-start | bytes 1179648
  16.5 2.5 %copy-start = (bf16[16,65536]{1,0:T(8,128)(2,1)S(1)}, bf16[16,65536]{1,0:T(8,128)(2,1)}, u32[]{:S(2)}) copy-start(bf16[16,65536]{1,0:T(8,128)(2,1)} %param.3) | copy-start | bytes 6291460
  123.0 15.6 %copy-start.1 = (f32[3]{0:T(128)}, f32[3]{0:T(128)S(1)}, u32[]{:S(2)}) copy-start(f32[3]{0:T(128)S(1)} %multiply_add_fusion) | copy-start | bytes 40
Sparse Core Ops, SparseCore 0:
  45.5 35.6 reduce-scatter.3
where the time goes:
time: 146 us; the launch traced here: 145 us
  blocking collectives  50.8 us (35%)
  waiting for transfers between devices  35.8 us (25%)
  matrix products  21.4 us (15%)
  between operations  16.1 us (11%)
  local copies, waits for them, and re-layouts  15 us (10%)
  other arithmetic  6.37 us (4%)
    psum x1, blocking collectives, body(): tile_counts = lax.psum(jnp.sum(owned_sums, axis=0), ('date', 'pix'))  37.4 us
    unnamed x2, waiting for transfers between devices  35.8 us
    dot_general x1, matrix products, block_counts(): jnp.einsum('ghdp,gldp->ghl', upper_table, lower_table, preferred_element_...  20.1 us
    all_gather x1, blocking collectives, body(): anomaly = lax.all_gather(owned_levels, 'date', axis=1, tiled=True)  13.3 us
    unnamed x8, local copies, waits for them, and re-layouts  5.39 us
    select_n x1, other arithmetic, block_counts(): upper_digit = chosen // 16  3.84 us
    dot_general x1, local copies, waits for them, and re-layouts, block_counts(): jnp.einsum('ghdp,gldp->ghl', upper_table, lower_table, preferred_element_...  3.23 us
  transfers between devices with their start and end apart: 1, of which 1 were waited for; matrix products, arithmetic and copies ran while one was open for 0% of the time, Pallas kernels for 0%

commit v1 on v0

--- a/solution.py
+++ b/solution.py
@@ -49,7 +49,7 @@
         scatter_dimension=0,
         tiled=True,
     )
-    tile_counts = lax.psum(jnp.sum(owned_sums, axis=0), ("date", "pix"))
+    tile_counts = lax.psum(lax.psum(jnp.sum(owned_sums, axis=0), "pix"), "date")
     tile_before = jnp.cumsum(tile_counts) - tile_counts
     tile_levels = percentiles(tile_counts[None], tile_before[None], jnp.sum(tile_counts)[None])[
         :, 0

time: 146 us -> 131 us (0.90)
  blocking collectives: 50.8 us -> 35.9 us
    psum x1 -> x2, blocking collectives: 37.4 us -> 23.1 us  [body(): tile_counts = lax.psum(lax.psum(jnp.sum(owned_sums, axis=0), 'pix'), 'date')]
where the time goes in v1:
time: 131 us
  blocking collectives  35.9 us (27%)
  waiting for transfers between devices  35.8 us (27%)
  matrix products  21.4 us (16%)
  between operations  16.1 us (12%)
  local copies, waits for them, and re-layouts  15 us (11%)
  other arithmetic  6.37 us (5%)
    unnamed x2, waiting for transfers between devices  35.8 us
    psum x2, blocking collectives, body(): tile_counts = lax.psum(lax.psum(jnp.sum(owned_sums, axis=0), 'pix'), 'date')  23.1 us
    dot_general x1, matrix products, block_counts(): jnp.einsum('ghdp,gldp->ghl', upper_table, lower_table, preferred_element_...  20.1 us
    all_gather x1, blocking collectives, body(): anomaly = lax.all_gather(owned_levels, 'date', axis=1, tiled=True)  12.8 us
    unnamed x8, local copies, waits for them, and re-layouts  5.39 us
    select_n x1, other arithmetic, block_counts(): upper_digit = chosen // 16  3.84 us
    dot_general x1, local copies, waits for them, and re-layouts, block_counts(): jnp.einsum('ghdp,gldp->ghl', upper_table, lower_table, preferred_element_...  3.23 us
  transfers between devices with their start and end apart: 1, of which 1 were waited for; matrix products, arithmetic and copies ran while one was open for 0% of the time, Pallas kernels for 0%

profile of v1, /device:TPU:0, one launch (start us, length us, event | category | flops | bytes accessed | tf_op | source)
XLA Modules:
  0.0 130.5 jit_solution(15436058891425254221)
XLA Ops:
  7.2 0.0 reduce-scatter.4.cloned.1.call-start
  7.2 3.0 %copy.40 = s32[2,8,512,128]{3,2,1,0:T(8,128)S(1)} copy(s32[2,8,512,128]{3,1,2,0:T(8,128)} %bitcast.84) | data formatting | bytes 8388608
  10.2 3.8 %add_select_fusion.1 = (s32[512,16,128]{2,0,1:T(8,128)S(1)}, s32[512,16,128]{2,0,1:T(8,128)S(1)}) fusion(s32[2,8,512,128]{3,2,1,0:T(8,128)S(1)} %copy.40), kind=kLoop, calls=%fused_computation.9 | loop fusion | flops 19922944 | bytes 12582912 | tf_op jit(solution)/shard_map/jit(floor_divide)/jit(_where)/select_n | solution.py:25
  14.1 2.4 %copy.29 = s32[512,16,128]{2,1,0:T(8,128)S(1)} copy(s32[512,16,128]{2,0,1:T(8,128)S(1)} %get-tuple-element.4) | data formatting | bytes 8388608 | tf_op jit(solution)/shard_map/jit(floor_divide)/jit(_where)/select_n | solution.py:25
  16.5 0.0 copy-start
  16.5 2.4 %copy.31 = s32[512,16,128]{2,1,0:T(8,128)S(1)} copy(s32[512,16,128]{2,0,1:T(8,128)S(1)} %get-tuple-element.5) | data formatting | bytes 8388608 | tf_op jit(solution)/shard_map/jit(remainder)/select_n | solution.py:26
  18.9 0.0 copy-done
  19.0 0.4 copy.41
  19.3 1.4 %copy.30 = bf16[512,16,128]{2,1,0:T(8,128)(2,1)S(1)} copy(bf16[512,16,128]{2,0,1:T(8,128)(2,1)S(1)} %bitcast.82) | data formatting | bytes 4194304 | tf_op jit(solution)/shard_map/transpose | solution.py:24
  20.7 20.1 %fusion.10 = f32[512,32,16]{1,2,0:T(8,128)} fusion(s32[512,16,128]{2,1,0:T(8,128)S(1)} %copy.31, s32[512,16,128]{2,1,0:T(8,128)S(1)} %copy.29, bf16[512,16,128]{2,1,0:T(8,128)(2,1)S(1)} %copy.30), kind=kOutput, calls=%fused_computation.18 | convolution fusion | flops 1157627904 | bytes 11534336 | tf_op jit(solution)/shard_map/ghdp,gldp->ghl/dot_general | solution.py:35
  40.8 3.2 %copy.32 = f32[512,32,16]{0,2,1:T(8,128)S(1)} copy(f32[512,32,16]{1,2,0:T(8,128)} %fusion.10) | data formatting | bytes 2097152 | tf_op jit(solution)/shard_map/ghdp,gldp->ghl/dot_general | solution.py:35
  44.0 1.3 %copy.36 = f32[512,512]{1,0:T(8,128)} copy(f32[512,512]{0,1:T(8,128)S(1)} %bitcast.83) | data formatting | bytes 2097152
  45.4 0.0 reduce-scatter.4.cloned.1.call-update
  45.4 35.8 %reduce-scatter.4.cloned.1.call-done = f32[64,512]{1,0:T(8,128)} async-done(((f32[512,512]{1,0:T(8,128)}), f32[64,512]{1,0:T(8,128)}) %reduce-scatter.4.cloned.1.call-update) | async-done | bytes 131088
  81.2 1.0 fusion.15
  82.2 9.5 %psum.14 = f32[512]{0:T(512)S(1)} all-reduce(f32[512]{0:T(512)S(1)} %get-tuple-element.2), channel_id=1, replica_groups=mesh['date'=8,'pix'=4] {'pix'}, use_global_device_ids=true, to_apply=%region_4.5 | all-reduce | flops 512 | bytes 4096 | tf_op jit(solution)/shard_map/psum | solution.py:52
  91.7 13.6 %psum.15 = f32[512]{0:T(512)S(1)} all-reduce(f32[512]{0:T(512)S(1)} %psum.14), channel_id=1, replica_groups=mesh['date'=8,'pix'=4] {'date'}, use_global_device_ids=true, to_apply=%region_5.6 | all-reduce | flops 512 | bytes 4096 | tf_op jit(solution)/shard_map/psum | solution.py:52
  105.3 0.3 reduce-window.9
  105.6 0.1 slice.7
  105.7 0.1 slice_reduce_fusion
  105.8 0.6 fusion.16
  108.4 0.1 maximum_bitcast_fusion
  108.5 0.2 clamp_reduce_fusion.1
  108.6 0.0 copy-start.1
  108.7 1.3 fusion.13
  109.9 0.2 clamp_reduce_fusion
  110.1 0.1 subtract_bitcast_fusion
  110.2 12.8 %all-gather = f32[8,64,3]{1,2,0:T(4,128)S(1)} all-gather(f32[1,64,3]{1,2,0:T(4,128)S(1)} %subtract_bitcast_fusion), channel_id=1, replica_groups=mesh['date'=8,'pix'=4] {'date'}, dimensions={0}, use_global_device_ids=true | all-gather | bytes 6912 | tf_op jit(solution)/shard_map/all_gather | solution.py:61
  123.0 0.7 reshape.186
  123.7 0.0 copy-done.1
  (5 shorter events, 0.1 us)
Async XLA Ops:
  7.2 74.0 %reduce-scatter.4.cloned.1.call-start = ((), (), s32[]{:S(2)}) async-start(), calls=%async_computation.1 | async-start | bytes 1179648
  16.5 2.5 %copy-start = (bf16[16,65536]{1,0:T(8,128)(2,1)S(1)}, bf16[16,65536]{1,0:T(8,128)(2,1)}, u32[]{:S(2)}) copy-start(bf16[16,65536]{1,0:T(8,128)(2,1)} %param.3) | copy-start | bytes 6291460
  108.6 15.0 %copy-start.1 = (f32[3]{0:T(128)}, f32[3]{0:T(128)S(1)}, u32[]{:S(2)}) copy-start(f32[3]{0:T(128)S(1)} %multiply_add_fusion) | copy-start | bytes 40
Sparse Core Ops, SparseCore 0:
  45.5 35.6 reduce-scatter.3

commit v2 on v0

--- a/solution.py
+++ b/solution.py
@@ -49,7 +49,7 @@
         scatter_dimension=0,
         tiled=True,
     )
-    tile_counts = lax.psum(jnp.sum(owned_sums, axis=0), ("date", "pix"))
+    tile_counts = jnp.sum(lax.all_gather(jnp.sum(owned_sums, axis=0), ("date", "pix")), axis=0)
     tile_before = jnp.cumsum(tile_counts) - tile_counts
     tile_levels = percentiles(tile_counts[None], tile_before[None], jnp.sum(tile_counts)[None])[
         :, 0

time: 146 us -> 174 us (1.19)
  blocking collectives: 50.8 us -> 78.5 us
    all_gather x0 -> x1, blocking collectives: none -> 65.7 us  [body(): lax.all_gather(jnp.sum(owned_sums, axis=0), ('date', 'pix'))]
    psum x1 -> x0, blocking collectives: 37.4 us -> none  [body(): tile_counts = lax.psum(jnp.sum(owned_sums, axis=0), ('date', 'pix'))]
where the time goes in v2:
time: 174 us; the launch traced here: 173 us
  blocking collectives  78.5 us (45%)
  waiting for transfers between devices  35.8 us (21%)
  matrix products  21.4 us (12%)
  between operations  16.1 us (9%)
  local copies, waits for them, and re-layouts  15 us (9%)
  other arithmetic  6.57 us (4%)
    all_gather x1, blocking collectives, body(): lax.all_gather(jnp.sum(owned_sums, axis=0), ('date', 'pix'))  65.7 us
    unnamed x2, waiting for transfers between devices  35.8 us
    dot_general x1, matrix products, block_counts(): jnp.einsum('ghdp,gldp->ghl', upper_table, lower_table, preferred_element_...  20.1 us
    all_gather x1, blocking collectives, body(): anomaly = lax.all_gather(owned_levels, 'date', axis=1, tiled=True)  12.8 us
    unnamed x8, local copies, waits for them, and re-layouts  5.39 us
    select_n x1, other arithmetic, block_counts(): upper_digit = chosen // 16  3.84 us
  transfers between devices with their start and end apart: 1, of which 1 were waited for; matrix products, arithmetic and copies ran while one was open for 0% of the time, Pallas kernels for 0%

profile of v2, /device:TPU:0, one launch (start us, length us, event | category | flops | bytes accessed | tf_op | source)
XLA Modules:
  0.0 173.4 jit_solution(3031015748234337034)
XLA Ops:
  7.2 0.0 reduce-scatter.4.cloned.1.call-start
  7.2 3.0 %copy.40 = s32[2,8,512,128]{3,2,1,0:T(8,128)S(1)} copy(s32[2,8,512,128]{3,1,2,0:T(8,128)} %bitcast.85) | data formatting | bytes 8388608
  10.2 3.8 %add_select_fusion.1 = (s32[512,16,128]{2,0,1:T(8,128)S(1)}, s32[512,16,128]{2,0,1:T(8,128)S(1)}) fusion(s32[2,8,512,128]{3,2,1,0:T(8,128)S(1)} %copy.40), kind=kLoop, calls=%fused_computation.9 | loop fusion | flops 19922944 | bytes 12582912 | tf_op jit(solution)/shard_map/jit(floor_divide)/jit(_where)/select_n | solution.py:25
  14.1 2.4 %copy.29 = s32[512,16,128]{2,1,0:T(8,128)S(1)} copy(s32[512,16,128]{2,0,1:T(8,128)S(1)} %get-tuple-element.6) | data formatting | bytes 8388608 | tf_op jit(solution)/shard_map/jit(floor_divide)/jit(_where)/select_n | solution.py:25
  16.5 0.0 copy-start
  16.5 2.4 %copy.31 = s32[512,16,128]{2,1,0:T(8,128)S(1)} copy(s32[512,16,128]{2,0,1:T(8,128)S(1)} %get-tuple-element.7) | data formatting | bytes 8388608 | tf_op jit(solution)/shard_map/jit(remainder)/select_n | solution.py:26
  18.9 0.0 copy-done
  19.0 0.4 copy.41
  19.3 1.4 copy.30
  20.7 20.1 %fusion.10 = f32[512,32,16]{1,2,0:T(8,128)} fusion(s32[512,16,128]{2,1,0:T(8,128)S(1)} %copy.31, s32[512,16,128]{2,1,0:T(8,128)S(1)} %copy.29, bf16[512,16,128]{2,1,0:T(8,128)(2,1)S(1)} %copy.30), kind=kOutput, calls=%fused_computation.18 | convolution fusion | flops 1157627904 | bytes 11534336 | tf_op jit(solution)/shard_map/ghdp,gldp->ghl/dot_general | solution.py:35
  40.8 3.2 %copy.32 = f32[512,32,16]{0,2,1:T(8,128)S(1)} copy(f32[512,32,16]{1,2,0:T(8,128)} %fusion.10) | data formatting | bytes 2097152 | tf_op jit(solution)/shard_map/ghdp,gldp->ghl/dot_general | solution.py:35
  44.0 1.3 copy.36
  45.4 0.0 reduce-scatter.4.cloned.1.call-update
  45.4 35.8 %reduce-scatter.4.cloned.1.call-done = f32[64,512]{1,0:T(8,128)} async-done(((f32[512,512]{1,0:T(8,128)}), f32[64,512]{1,0:T(8,128)}) %reduce-scatter.4.cloned.1.call-update) | async-done | bytes 131088
  81.2 1.0 fusion.15
  82.2 65.7 %all-gather.1 = f32[32,1,512]{2,1,0:T(1,128)S(1)} all-gather(f32[1,1,512]{2,1,0:T(1,128)S(1)} %bitcast.88), channel_id=2, replica_groups=mesh['date'=8,'pix'=4] {'date','pix'}, dimensions={0}, use_global_device_ids=true | all-gather | bytes 67584 | tf_op jit(solution)/shard_map/all_gather | solution.py:52
  147.9 0.7 fusion.16
  150.6 0.3 reduce-window.9
  150.9 0.1 slice.7
  151.0 0.1 slice_reduce_fusion
  151.1 0.1 bitcast_subtract_fusion
  151.2 0.1 maximum_bitcast_fusion
  151.3 0.2 clamp_reduce_fusion.1
  151.5 0.0 copy-start.1
  151.5 1.3 fusion.13
  152.8 0.2 clamp_reduce_fusion
  153.0 0.1 subtract_bitcast_fusion
  153.1 12.8 %all-gather.2 = f32[8,64,3]{1,2,0:T(4,128)S(1)} all-gather(f32[1,64,3]{1,2,0:T(4,128)S(1)} %subtract_bitcast_fusion), channel_id=1, replica_groups=mesh['date'=8,'pix'=4] {'date'}, dimensions={0}, use_global_device_ids=true | all-gather | bytes 6912 | tf_op jit(solution)/shard_map/all_gather | solution.py:61
  165.8 0.7 reshape.206
  166.5 0.0 copy-done.1
  (5 shorter events, 0.1 us)
Async XLA Ops:
  7.2 74.0 %reduce-scatter.4.cloned.1.call-start = ((), (), s32[]{:S(2)}) async-start(), calls=%async_computation.1 | async-start | bytes 1179648
  16.5 2.5 %copy-start = (bf16[16,65536]{1,0:T(8,128)(2,1)S(1)}, bf16[16,65536]{1,0:T(8,128)(2,1)}, u32[]{:S(2)}) copy-start(bf16[16,65536]{1,0:T(8,128)(2,1)} %param.3) | copy-start | bytes 6291460
  151.5 15.0 %copy-start.1 = (f32[3]{0:T(128)}, f32[3]{0:T(128)S(1)}, u32[]{:S(2)}) copy-start(f32[3]{0:T(128)S(1)} %multiply_add_fusion) | copy-start | bytes 40
Sparse Core Ops, SparseCore 0:
  45.5 35.6 reduce-scatter.3
